TPU v7x, 32 devices: a whole 2x2x4 slice. The times are simulated.
32 devices in a mesh: dp: 2 (over y), ep: 16 (over z, x, core).
Axes of the slice: x: 2, y: 2, z: 4, core: 2. Of those that a mesh axis runs over, the one named last changes fastest.
Arguments:
- hidden_in: bfloat16 [768, 4096], P(('dp', 'ep')), may hold values from -6 to 6
- expert_ids: int32 [768, 2], P(('dp', 'ep')), may hold values from 0 to 15, all different within a row; in each aligned block of 24 rows (0 to 23, 24 to 47, ...) at most 4 rows name the same one
- route_logits: float32 [768, 16], P(('dp', 'ep')), may hold values from -10 to 10
- first_weight: bfloat16 [16, 4096, 1024], P('ep', None, 'dp'), may hold values from -0.09375 to 0.09375
- second_weight: bfloat16 [16, 1024, 4096], P('ep', None, 'dp'), may hold values from -0.1875 to 0.1875
- queries: bfloat16 [768, 2048], P(('dp', 'ep')), may hold values from -140 to 140
- span_keys: bfloat16 [768, 2048], P(('dp', 'ep')), may hold values from -7 to 7
- span_values: bfloat16 [768, 2048], P(('dp', 'ep')), may hold values from -6 to 6
- cache_keys: bfloat16 [32, 72, 2048], P(('dp', 'ep')), may hold values from -6 to 6
- cache_values: bfloat16 [32, 72, 2048], P(('dp', 'ep')), may hold values from -6 to 6
- valid_frames: int32 [32], P(('dp', 'ep')), may hold values from 1 to 3
Outputs:
- mixed: bfloat16 [768, 4096], P(('dp', 'ep'))
- attended: bfloat16 [768, 2048], P(('dp', 'ep'))
Inputs may be any that keep to these rules, and one draw needn't show every extreme that they name: `expert_ids`: each token names two different experts. In the rows of one device (24 rows) no expert is named more than 4 times, a bound that some block reaches.
All inputs are finite; a program needn't handle non-finite values.
Results may differ from a plain program's by a relative error of at most 0.0057.
Values may be sent and summed in bfloat16 or wider, within the bound.
A program may use at most 128 MiB of HBM per device.

v0:
```python
import functools
import math

import jax
import jax.numpy as jnp
from jax import lax
from jax.experimental import pallas as pl
from jax.experimental.pallas import tpu as pltpu
from jax.sharding import PartitionSpec as P

HEAD_DIM = 128
FRAME_TOK = 24
TILE = 16
MESH = pl.DeviceIdType.MESH


def iota(shape, axis):
    return lax.broadcasted_iota(jnp.int32, shape, axis)


def as_bf16(mask):
    return jnp.where(mask, 1.0, 0.0).astype(jnp.bfloat16)


def log2(n):
    return n.bit_length() - 1


def flip(me, off, n):
    out = jnp.int32(0)
    bit = 1
    while bit < n:
        one = jnp.int32(bit)
        out = out + one * lax.rem(lax.div(me, one) + lax.div(off, one), jnp.int32(2))
        bit *= 2
    return out


def fold_map(shape, long_axis, group, cap):
    long, tiled = iota(shape, long_axis), iota(shape, 1 - long_axis)
    fold = long >> log2(group * cap)
    source = (long & (group * cap - 1)) >> log2(cap)
    slot = long & (cap - 1)
    return as_bf16(tiled == source * TILE + fold * cap + slot)


def dot(a, b):
    return jnp.dot(a, b, preferred_element_type=jnp.float32)


def drain(view, sem):
    pltpu.make_async_copy(view, view, sem).wait()


def attend(q, k, v, ck, cv, frames, out):
    cache_len = ck.shape[0]
    scale = 1.0 / math.sqrt(HEAD_DIM)
    usable = (iota((1, cache_len), 1) // FRAME_TOK) < frames
    contract = (((1,), (1,)), ((), ()))
    for head in range(q.shape[1] // HEAD_DIM):
        cols = slice(head * HEAD_DIM, (head + 1) * HEAD_DIM)
        query = q[:, cols]
        old = lax.dot_general(query, ck[:, cols], contract, preferred_element_type=jnp.float32)
        new = lax.dot_general(query, k[:, cols], contract, preferred_element_type=jnp.float32)
        old = jnp.where(usable, old * scale, -1e30)
        new = new * scale
        top = jnp.maximum(
            jnp.max(old, axis=1, keepdims=True), jnp.max(new, axis=1, keepdims=True)
        )
        old = jnp.exp(old - top)
        new = jnp.exp(new - top)
        total = jnp.sum(old, axis=1, keepdims=True) + jnp.sum(new, axis=1, keepdims=True)
        old = (old / total).astype(jnp.bfloat16)
        new = (new / total).astype(jnp.bfloat16)
        out[:, cols] = (dot(old, cv[:, cols]) + dot(new, v[:, cols])).astype(jnp.bfloat16)


def kernel(
    dp_n, ep_n, passes, cap, back_folds,
    frames, ids_hbm, logits_hbm, hidden_hbm,
    q_hbm, k_hbm, v_hbm, ck_hbm, cv_hbm, w1_hbm, w2_hbm,
    mixed, attended,
    ids, logits, hidden, w1, w2, q, k, v, ck, cv,
    disp, rows, xs, hid, ys, back_out, back_in,
    load_sem, disp_send, disp_recv, relay_send, relay_recv,
    hid_send, hid_recv, back_send, back_recv, own_sem,
):
    d, me = lax.axis_index("dp"), lax.axis_index("ep")
    tokens = hidden.shape[0]
    folds = TILE // cap
    fold_cols = disp.shape[2]
    back_cols = back_in.shape[2]
    group = min(ep_n, 16)
    group_rows = group * cap
    total = dp_n * ep_n

    barrier = pltpu.get_barrier_semaphore()

    def greet(i, carry):
        pl.semaphore_signal(
            barrier, inc=1, device_id={"dp": d, "ep": flip(me, i, ep_n)}, device_id_type=MESH
        )
        return carry

    lax.fori_loop(1, ep_n, greet, 0)
    for i in range(1, dp_n):
        pl.semaphore_signal(
            barrier,
            inc=1,
            device_id={"dp": lax.rem(d + i, jnp.int32(dp_n)), "ep": me},
            device_id_type=MESH,
        )

    loads = [
        pltpu.make_async_copy(src, dst, load_sem.at[i])
        for i, (src, dst) in enumerate(
            [
                (ids_hbm, ids), (logits_hbm, logits), (hidden_hbm, hidden),
                (w1_hbm, w1), (w2_hbm, w2),
                (q_hbm, q), (k_hbm, k), (v_hbm, v), (ck_hbm, ck), (cv_hbm, cv),
            ]
        )
    ]
    for load in loads:
        load.start()
    for load in loads[:3]:
        load.wait()

    experts = iota((ep_n, tokens), 0)
    named = [experts == ids[c : c + 1, :] for c in range(2)]
    count = as_bf16(named[0] | named[1])
    earlier = as_bf16(iota((tokens, tokens), 0) < iota((tokens, tokens), 1))
    before = dot(count, earlier)
    eye = iota((tokens, tokens), 0) == iota((tokens, tokens), 1)
    place, place_row, chosen = [], [], []
    for c in range(2):
        slot = jnp.sum(jnp.where(named[c], before, 0.0), axis=0, keepdims=True).astype(jnp.int32)
        turn = slot >> log2(cap)
        place_row.append((turn * ep_n + ids[c : c + 1, :]) * TILE + (slot & (cap - 1)))
        place.append(jnp.sum(jnp.where(eye, place_row[c], 0), axis=1, keepdims=True))
        chosen.append(jnp.sum(jnp.where(named[c], logits[...], 0.0), axis=0, keepdims=True))
    top = jnp.maximum(chosen[0], chosen[1])
    powers = [jnp.exp(x - top) for x in chosen]
    gates = [
        jnp.sum(jnp.where(eye, p / (powers[0] + powers[1]), 0.0), axis=1, keepdims=True)
        for p in powers
    ]

    row_at = iota((passes * ep_n * TILE, tokens), 0)
    pickers = [
        as_bf16((row_at - f * cap == place_row[0]) | (row_at - f * cap == place_row[1]))
        for f in range(folds)
    ]
    step = min(fold_cols, 256)
    for at in range(0, fold_cols, step):
        acc = dot(pickers[0], hidden[:, at : at + step])
        for f in range(1, folds):
            acc += dot(pickers[f], hidden[:, f * fold_cols + at : f * fold_cols + at + step])
        disp[:, :, at : at + step] = acc.astype(jnp.bfloat16).reshape(passes * ep_n, TILE, step)

    pl.semaphore_wait(barrier, ep_n + dp_n - 2)

    for turn in range(passes):

        def dispatch(off, carry):
            target = flip(me, off, ep_n)
            pltpu.make_async_remote_copy(
                src_ref=disp.at[turn * ep_n + target],
                dst_ref=rows.at[turn * total + d * ep_n + me],
                send_sem=disp_send,
                recv_sem=disp_recv.at[turn * ep_n + me],
                device_id={"dp": d, "ep": target},
                device_id_type=MESH,
            ).start()
            return carry

        lax.fori_loop(1, ep_n, dispatch, 0)
        pltpu.make_async_copy(
            disp.at[turn * ep_n + me],
            rows.at[turn * total + d * ep_n + me],
            disp_recv.at[turn * ep_n + me],
        ).start()

    def relay(turn, first, last):
        def one(off, carry):
            source = flip(me, off, ep_n)
            chunk = rows.at[turn * total + d * ep_n + source]
            drain(chunk, disp_recv.at[turn * ep_n + source])
            for j in range(1, dp_n):
                pltpu.make_async_remote_copy(
                    src_ref=chunk,
                    dst_ref=chunk,
                    send_sem=relay_send,
                    recv_sem=relay_recv.at[turn * dp_n + d],
                    device_id={"dp": lax.rem(d + j, jnp.int32(dp_n)), "ep": me},
                    device_id_type=MESH,
                ).start()
            return carry

        lax.fori_loop(first, last, one, 0)

    unfold = fold_map((folds * group_rows, group * TILE), 0, group, cap)
    refold = fold_map((group * TILE, back_folds * group_rows), 1, group, cap)

    def first(turn, j):
        plane = lax.rem(d + j, jnp.int32(dp_n))
        if j > 0:
            drain(rows.at[pl.ds(turn * total + plane * ep_n, ep_n)], relay_recv.at[turn * dp_n + plane])
        for g in range(ep_n // group):
            tiles = rows[pl.ds(turn * total + plane * ep_n + g * group, group)].reshape(group * TILE, fold_cols)
            flat = dot(unfold, tiles).astype(jnp.bfloat16)
            for f in range(folds):
                xs[f, g * group_rows : (g + 1) * group_rows, :] = flat[
                    f * group_rows : (f + 1) * group_rows
                ]
        acc = dot(xs[0], w1[:fold_cols, :])
        for f in range(1, folds):
            acc += dot(xs[f], w1[f * fold_cols : (f + 1) * fold_cols, :])
        hid[(turn * dp_n + plane) * dp_n + d] = jax.nn.gelu(acc, approximate=True).astype(jnp.bfloat16)
        for i in range(1, dp_n):
            pltpu.make_async_remote_copy(
                src_ref=hid.at[(turn * dp_n + plane) * dp_n + d],
                dst_ref=hid.at[(turn * dp_n + plane) * dp_n + d],
                send_sem=hid_send,
                recv_sem=hid_recv.at[(turn * dp_n + plane) * dp_n + d],
                device_id={"dp": lax.rem(d + i, jnp.int32(dp_n)), "ep": me},
                device_id_type=MESH,
            ).start()

    units = hid.shape[2]

    def second(turn, j):
        plane = lax.rem(d + j, jnp.int32(dp_n))
        for i in range(1, dp_n):
            part = (turn * dp_n + plane) * dp_n + lax.rem(d + i, jnp.int32(dp_n))
            drain(hid.at[part], hid_recv.at[part])
        for f in range(back_folds):
            cols = slice(f * back_cols, (f + 1) * back_cols)
            acc = dot(hid[(turn * dp_n + plane) * dp_n], w2[:units, cols])
            for i in range(1, dp_n):
                acc += dot(hid[(turn * dp_n + plane) * dp_n + i], w2[i * units : (i + 1) * units, cols])
            ys[f] = acc.astype(jnp.bfloat16)
        for g in range(ep_n // group):
            flat = jnp.concatenate(
                [ys[f, g * group_rows : (g + 1) * group_rows, :] for f in range(back_folds)], axis=0
            )
            tiles = dot(refold, flat).astype(jnp.bfloat16)
            back_out[pl.ds(turn * total + plane * ep_n + g * group, group)] = tiles.reshape(group, TILE, back_cols)

        def give_back(off, carry):
            target = flip(me, off, ep_n)
            pltpu.make_async_remote_copy(
                src_ref=back_out.at[turn * total + plane * ep_n + target],
                dst_ref=back_in.at[turn * total + d * ep_n + me],
                send_sem=back_send,
                recv_sem=back_recv,
                device_id={"dp": plane, "ep": target},
                device_id_type=MESH,
            ).start()
            return carry

        lax.fori_loop(1 if j == 0 else 0, ep_n, give_back, 0)
        if j == 0:
            pltpu.make_async_copy(
                back_out.at[turn * total + d * ep_n + me], back_in.at[turn * total + d * ep_n + me], own_sem
            ).start()

    planes = range(dp_n)
    relay(0, 0, ep_n)
    loads[3].wait()
    first(0, 0)
    if passes > 1:
        relay(1, 0, ep_n // 2)
    for j in planes[1:]:
        first(0, j)
    if passes > 1:
        relay(1, ep_n // 2, ep_n)
        first(1, 0)
    loads[4].wait()
    second(0, 0)
    if passes > 1:
        for j in planes[1:]:
            first(1, j)
    for j in planes[1:]:
        second(0, j)
    if passes > 1:
        for j in planes:
            second(1, j)

    for load in loads[5:]:
        load.wait()
    attend(q, k, v, ck, cv, frames[0], attended)

    col_at = iota((tokens, passes * ep_n * TILE), 1)
    picks = jnp.concatenate(
        [
            jnp.where(col_at - f * cap == place[c], 1.0, 0.0)
            for f in range(back_folds)
            for c in range(2)
        ],
        axis=0,
    ).astype(jnp.bfloat16)

    drain(back_in.at[pl.ds(0, passes * (total - 1))], back_recv)
    drain(back_in.at[pl.ds(0, passes)], own_sem)
    for h in range(dp_n):
        starts = [turn * total + h * ep_n for turn in range(passes)]
        tiles = jnp.concatenate(
            [back_in[at : at + ep_n].reshape(ep_n * TILE, back_cols) for at in starts], axis=0
        )
        picked = dot(picks, tiles)
        for f in range(back_folds):
            at = 2 * f * tokens
            cols = slice((h * back_folds + f) * back_cols, (h * back_folds + f + 1) * back_cols)
            mixed[:, cols] = (
                gates[0] * picked[at : at + tokens] + gates[1] * picked[at + tokens : at + 2 * tokens]
            ).astype(jnp.bfloat16)

    drain(disp.at[pl.ds(0, passes * (ep_n - 1))], disp_send)
    if dp_n > 1:
        drain(rows.at[pl.ds(0, passes * (dp_n - 1) * ep_n)], relay_send)
        drain(hid.at[pl.ds(0, passes * dp_n * (dp_n - 1))], hid_send)
    drain(back_out.at[pl.ds(0, passes * (total - 1))], back_send)


def shards(dp_n, ep_n, *args):
    (hidden_in, expert_ids, route_logits, first_weight, second_weight,
     queries, span_keys, span_values, cache_keys, cache_values, valid_frames) = args
    tokens, width = hidden_in.shape
    cap = max(2, 8 * tokens // (3 * ep_n))
    passes = 2 if cap % 4 == 0 else 1
    cap //= passes
    _, _, units = first_weight.shape
    _, all_units, cols = second_weight.shape
    folds = TILE // cap
    back_folds = min(folds, cols // 128)
    slots = ep_n * cap
    bf16 = jnp.bfloat16
    vmem, hbm = pl.BlockSpec(memory_space=pltpu.VMEM), pl.BlockSpec(memory_space=pltpu.HBM)
    dma = pltpu.SemaphoreType.DMA
    total = dp_n * ep_n
    streamed = (
        expert_ids.T, route_logits.T, hidden_in,
        queries, span_keys, span_values, cache_keys[0], cache_values[0],
        first_weight[0], second_weight[0],
    )
    return pl.pallas_call(
        functools.partial(kernel, dp_n, ep_n, passes, cap, back_folds),
        out_shape=(
            jax.ShapeDtypeStruct((tokens, width), bf16),
            jax.ShapeDtypeStruct(queries.shape, bf16),
        ),
        in_specs=[pl.BlockSpec(memory_space=pltpu.SMEM)] + [hbm] * len(streamed),
        out_specs=(vmem, vmem),
        scratch_shapes=[
            pltpu.VMEM((2, tokens), jnp.int32),
            pltpu.VMEM((ep_n, tokens), jnp.float32),
            pltpu.VMEM((tokens, width), bf16),
            pltpu.VMEM((width, units), bf16),
            pltpu.VMEM((all_units, cols), bf16),
            pltpu.VMEM(queries.shape, bf16),
            pltpu.VMEM(span_keys.shape, bf16),
            pltpu.VMEM(span_values.shape, bf16),
            pltpu.VMEM(cache_keys.shape[1:], bf16),
            pltpu.VMEM(cache_values.shape[1:], bf16),
            pltpu.VMEM((passes * ep_n, TILE, width // folds), bf16),
            pltpu.VMEM((passes * total, TILE, width // folds), bf16),
            pltpu.VMEM((folds, slots, width // folds), bf16),
            pltpu.VMEM((passes * dp_n * dp_n, slots, units), bf16),
            pltpu.VMEM((back_folds, slots, cols // back_folds), bf16),
            pltpu.VMEM((passes * total, TILE, cols // back_folds), bf16),
            pltpu.VMEM((passes * total, TILE, cols // back_folds), bf16),
            dma((len(streamed),)),
            dma(()),
            dma((passes * ep_n,)),
            dma(()),
            dma((passes * dp_n,)),
            dma(()),
            dma((passes * dp_n * dp_n,)),
            dma(()),
            dma(()),
            dma(()),
        ],
        compiler_params=pltpu.CompilerParams(
            collective_id=0, has_side_effects=True, vmem_limit_bytes=40 * 1024 * 1024
        ),
    )(
        valid_frames,
        *[pltpu.with_memory_space_constraint(x, pltpu.HBM) for x in streamed],
    )


def solution(mesh):
    tokens = P(("dp", "ep"), None)
    weights = P("ep", None, "dp")
    cache = P(("dp", "ep"), None, None)
    return jax.shard_map(
        functools.partial(shards, mesh.shape["dp"], mesh.shape["ep"]),
        mesh=mesh,
        in_specs=(
            tokens, tokens, tokens, weights, weights, tokens, tokens, tokens, cache, cache,
            P(("dp", "ep")),
        ),
        out_specs=(tokens, tokens),
        check_vma=False,
    )
```

profile of v0, /device:TPU:0, one launch (start us, length us, event | category | flops | bytes accessed | tf_op | source)
XLA Modules:
  0.0 41.1 jit_solution(4179829746578346515)
XLA Ops:
  1.3 38.4 %shard_map.122 = (bf16[24,4096]{1,0:T(8,128)(2,1)S(1)}, bf16[24,2048]{1,0:T(8,128)(2,1)S(1)}) custom-call(s32[1]{0:T(128)S(6)} %copy.15.frames, s32[2,24]{1,0:T(2,128)} %bitcast.11, f32[16,24]{1,0:T(8,128)} %bitcast.10, bf16[24,4096]{1,0:T(8,128)(2,1)} %hidden_hbm.1, bf16[24,2048]{1,0:T(8,128)(2,1)} %q_hbm.1, bf16[24,2048]{1,0:T(8,128)(2,1)} %k_hbm.1, ...), custom_call_target="tpu_custom_call" | custom-call | tf_op jit(solution)/shard_map/pallas_call | solution.py:347
  39.7 0.7 %copy.16 = bf16[24,4096]{1,0:T(8,128)(2,1)} copy(bf16[24,4096]{1,0:T(8,128)(2,1)S(1)} %get-tuple-element.4) | data formatting | bytes 393216
  40.4 0.6 %copy.17 = bf16[24,2048]{1,0:T(8,128)(2,1)} copy(bf16[24,2048]{1,0:T(8,128)(2,1)S(1)} %get-tuple-element.5) | data formatting | bytes 196608
where the time goes:
time: 41.2 us; the launch traced here: 41.1 us
  Pallas kernels  38.4 us (93%)
  local copies, waits for them, and re-layouts  1.32 us (3%)
  between operations  1.29 us (3%)
    pallas_call x1, Pallas kernels, shards(): pl.pallas_call(functools.partial(kernel, dp_n, ep_n, passes, cap, back_fo...  38.4 us
    unnamed x2, local copies, waits for them, and re-layouts  1.32 us

commit v1 on v0

v1 whole, which is shorter than its diff:
```python
import functools
import math

import jax
import jax.numpy as jnp
from jax import lax
from jax.experimental import pallas as pl
from jax.experimental.pallas import tpu as pltpu
from jax.sharding import PartitionSpec as P

HEAD_DIM = 128
FRAME_TOK = 24
TILE = 16
WAVES = 4
MESH = pl.DeviceIdType.MESH


def iota(shape, axis):
    return lax.broadcasted_iota(jnp.int32, shape, axis)


def as_bf16(mask):
    return jnp.where(mask, 1.0, 0.0).astype(jnp.bfloat16)


def log2(n):
    return n.bit_length() - 1


def fold_map(shape, long_axis, group, cap):
    long, tiled = iota(shape, long_axis), iota(shape, 1 - long_axis)
    fold = long >> log2(group * cap)
    source = (long & (group * cap - 1)) >> log2(cap)
    slot = long & (cap - 1)
    return as_bf16(tiled == source * TILE + fold * cap + slot)


def dot(a, b):
    return jnp.dot(a, b, preferred_element_type=jnp.float32)


def drain(view, sem):
    pltpu.make_async_copy(view, view, sem).wait()


def loop(low, high, body):
    if high - low <= 8:
        for i in range(low, high):
            body(i)
    else:
        lax.fori_loop(low, high, lambda i, carry: (body(i), carry)[1], 0)


def attend(q, k, v, ck, cv, frames, out, head):
    cache_len = ck.shape[0]
    scale = 1.0 / math.sqrt(HEAD_DIM)
    usable = (iota((1, cache_len), 1) // FRAME_TOK) < frames
    contract = (((1,), (1,)), ((), ()))
    cols = slice(head * HEAD_DIM, (head + 1) * HEAD_DIM)
    query = q[:, cols]
    old = lax.dot_general(query, ck[:, cols], contract, preferred_element_type=jnp.float32)
    new = lax.dot_general(query, k[:, cols], contract, preferred_element_type=jnp.float32)
    old = jnp.where(usable, old * scale, -1e30)
    new = new * scale
    top = jnp.maximum(
        jnp.max(old, axis=1, keepdims=True), jnp.max(new, axis=1, keepdims=True)
    )
    old = jnp.exp(old - top)
    new = jnp.exp(new - top)
    total = jnp.sum(old, axis=1, keepdims=True) + jnp.sum(new, axis=1, keepdims=True)
    old = (old / total).astype(jnp.bfloat16)
    new = (new / total).astype(jnp.bfloat16)
    out[:, cols] = (dot(old, cv[:, cols]) + dot(new, v[:, cols])).astype(jnp.bfloat16)


def kernel(
    dp_n, ep_n, cap, back_folds,
    frames, ids_hbm, logits_hbm, hidden_hbm,
    q_hbm, k_hbm, v_hbm, ck_hbm, cv_hbm, w1_hbm, w2_hbm,
    mixed, attended,
    ids, logits, hidden, w1, w2, q, k, v, ck, cv,
    disp, rows, xs, hid, ys, back_out, back_in,
    load_sem, disp_send, disp_recv, relay_send, relay_recv,
    hid_send, hid_recv, back_send, back_recv, own_sem,
):
    d, me = lax.axis_index("dp"), lax.axis_index("ep")
    tokens = hidden.shape[0]
    folds = TILE // cap
    fold_cols = disp.shape[2]
    back_cols = back_in.shape[2]
    total = dp_n * ep_n
    wave = ep_n // WAVES
    per, half = wave // 2, ep_n // 2
    slots = wave * cap
    own = per
    units = hid.shape[2]

    bits = [lax.rem(lax.div(me, jnp.int32(1 << b)), jnp.int32(2)) for b in range(log2(ep_n))]

    def partner(off):
        both = jnp.int32(0)
        for b, bit in enumerate(bits):
            both = both + (bit * ((off // (1 << b)) % 2)) * (1 << b)
        return me + off - 2 * both

    barrier = pltpu.get_barrier_semaphore()

    loads = [
        pltpu.make_async_copy(src, dst, load_sem.at[i])
        for i, (src, dst) in enumerate(
            [
                (ids_hbm, ids), (logits_hbm, logits), (hidden_hbm, hidden),
                (q_hbm, q), (k_hbm, k), (v_hbm, v), (ck_hbm, ck), (cv_hbm, cv),
                (w1_hbm, w1), (w2_hbm, w2),
            ]
        )
    ]
    for load in loads:
        load.start()

    def greet(off):
        pl.semaphore_signal(
            barrier, inc=1, device_id={"dp": d, "ep": partner(off)}, device_id_type=MESH
        )

    loop(1, ep_n, greet)
    for i in range(1, dp_n):
        pl.semaphore_signal(
            barrier,
            inc=1,
            device_id={"dp": lax.rem(d + i, jnp.int32(dp_n)), "ep": me},
            device_id_type=MESH,
        )
    for load in loads[:3]:
        load.wait()

    experts = iota((ep_n, tokens), 0)
    named = [experts == ids[c : c + 1, :] for c in range(2)]
    count = as_bf16(named[0] | named[1])
    earlier = as_bf16(iota((tokens, tokens), 0) < iota((tokens, tokens), 1))
    before = dot(count, earlier)
    eye = iota((tokens, tokens), 0) == iota((tokens, tokens), 1)
    place_row = []
    for c in range(2):
        slot = jnp.sum(jnp.where(named[c], before, 0.0), axis=0, keepdims=True).astype(jnp.int32)
        off = ids[c : c + 1, :] ^ me
        inner = off & (half - 1)
        at = (inner >> log2(per)) * wave + (inner & (per - 1)) + jnp.where(off < half, per, 0)
        place_row.append(at * TILE + slot)

    row_at = iota((wave * TILE, tokens), 0)

    def pick(w):
        pickers = [
            as_bf16(
                (row_at + (w * wave * TILE - f * cap) == place_row[0])
                | (row_at + (w * wave * TILE - f * cap) == place_row[1])
            )
            for f in range(folds)
        ]
        step = min(fold_cols, 256)
        for at in range(0, fold_cols, step):
            acc = dot(pickers[0], hidden[:, at : at + step])
            for f in range(1, folds):
                acc += dot(pickers[f], hidden[:, f * fold_cols + at : f * fold_cols + at + step])
            disp[w * wave : (w + 1) * wave, :, at : at + step] = acc.astype(jnp.bfloat16).reshape(
                wave, TILE, step
            )

    def send(p, off):
        pltpu.make_async_remote_copy(
            src_ref=disp.at[p],
            dst_ref=rows.at[d * ep_n + p],
            send_sem=disp_send,
            recv_sem=disp_recv.at[p],
            device_id={"dp": d, "ep": partner(off)},
            device_id_type=MESH,
        ).start()

    def pass_on(p, source):
        for j in range(1, dp_n):
            pltpu.make_async_remote_copy(
                src_ref=source,
                dst_ref=rows.at[d * ep_n + p],
                send_sem=relay_send,
                recv_sem=relay_recv.at[(p // wave) * dp_n + d],
                device_id={"dp": lax.rem(d + j, jnp.int32(dp_n)), "ep": me},
                device_id_type=MESH,
            ).start()

    def dispatch(w):
        loop(0, per, lambda i: send(w * wave + i, half + w * per + i))
        loop(1 if w == 0 else 0, per, lambda i: send(w * wave + per + i, w * per + i))
        if w == 0:
            pltpu.make_async_copy(disp.at[own], rows.at[d * ep_n + own], disp_recv.at[own]).start()
            pass_on(own, disp.at[own])

    def relay(w):
        def one(p):
            chunk = rows.at[d * ep_n + p]
            drain(chunk, disp_recv.at[p])
            pass_on(p, chunk)

        if w == 0:
            drain(rows.at[d * ep_n + own], disp_recv.at[own])
        loop(1 if w == 0 else 0, per, lambda i: one(w * wave + per + i))
        loop(0, per, lambda i: one(w * wave + i))

    unfold = fold_map((folds * slots, wave * TILE), 0, wave, cap)
    refold = fold_map((wave * TILE, back_folds * slots), 1, wave, cap)

    def first(w):
        for j in range(1, dp_n):
            plane = lax.rem(d + j, jnp.int32(dp_n))
            drain(rows.at[pl.ds(plane * ep_n + w * wave, wave)], relay_recv.at[w * dp_n + plane])
        for plane in range(dp_n):
            at = plane * ep_n + w * wave
            flat = dot(unfold, rows[at : at + wave].reshape(wave * TILE, fold_cols)).astype(jnp.bfloat16)
            for f in range(folds):
                xs[f, plane * slots : (plane + 1) * slots, :] = flat[f * slots : (f + 1) * slots]
        acc = dot(xs[0], w1[:fold_cols, :])
        for f in range(1, folds):
            acc += dot(xs[f], w1[f * fold_cols : (f + 1) * fold_cols, :])
        hid[w * dp_n + d] = jax.nn.gelu(acc, approximate=True).astype(jnp.bfloat16)
        for i in range(1, dp_n):
            pltpu.make_async_remote_copy(
                src_ref=hid.at[w * dp_n + d],
                dst_ref=hid.at[w * dp_n + d],
                send_sem=hid_send,
                recv_sem=hid_recv.at[w * dp_n + d],
                device_id={"dp": lax.rem(d + i, jnp.int32(dp_n)), "ep": me},
                device_id_type=MESH,
            ).start()

    def second(w):
        for i in range(1, dp_n):
            part = w * dp_n + lax.rem(d + i, jnp.int32(dp_n))
            drain(hid.at[part], hid_recv.at[part])
        for f in range(back_folds):
            cols = slice(f * back_cols, (f + 1) * back_cols)
            acc = dot(hid[w * dp_n], w2[:units, cols])
            for i in range(1, dp_n):
                acc += dot(hid[w * dp_n + i], w2[i * units : (i + 1) * units, cols])
            ys[f] = acc.astype(jnp.bfloat16)
        for plane in range(dp_n):
            flat = jnp.concatenate(
                [ys[f, plane * slots : (plane + 1) * slots, :] for f in range(back_folds)], axis=0
            )
            tiles = dot(refold, flat).astype(jnp.bfloat16)
            at = plane * ep_n + w * wave
            back_out[at : at + wave] = tiles.reshape(wave, TILE, back_cols)

        def give(p, off):
            for j in range(dp_n):
                plane = lax.rem(d + j, jnp.int32(dp_n))
                if isinstance(off, int) and off == 0 and j == 0:
                    continue
                pltpu.make_async_remote_copy(
                    src_ref=back_out.at[plane * ep_n + p],
                    dst_ref=back_in.at[d * ep_n + p],
                    send_sem=back_send,
                    recv_sem=back_recv,
                    device_id={"dp": plane, "ep": partner(off)},
                    device_id_type=MESH,
                ).start()

        loop(0, per, lambda i: give(w * wave + i, half + w * per + i))
        if w == 0:
            give(own, 0)
            pltpu.make_async_copy(
                back_out.at[d * ep_n + own], back_in.at[d * ep_n + own], own_sem
            ).start()
        loop(1 if w == 0 else 0, per, lambda i: give(w * wave + per + i, w * per + i))

    waiting = list(range(q.shape[1] // HEAD_DIM))

    def heads(n):
        for _ in range(min(n, len(waiting))):
            attend(q, k, v, ck, cv, frames[0], attended, waiting.pop(0))

    pick(0)
    pl.semaphore_wait(barrier, ep_n + dp_n - 2)
    dispatch(0)
    for w in range(1, WAVES):
        pick(w)
        dispatch(w)
    for load in loads[3:8]:
        load.wait()
    heads(8)
    relay(0)
    heads(4)
    relay(1)
    loads[8].wait()
    first(0)
    heads(2)
    relay(2)
    first(1)
    loads[9].wait()
    second(0)
    relay(3)
    first(2)
    second(1)
    first(3)
    second(2)
    heads(1)
    second(3)
    heads(len(waiting))

    chosen = [
        jnp.sum(jnp.where(named[c], logits[...], 0.0), axis=0, keepdims=True) for c in range(2)
    ]
    top = jnp.maximum(chosen[0], chosen[1])
    powers = [jnp.exp(x - top) for x in chosen]
    gates = [
        jnp.sum(jnp.where(eye, p / (powers[0] + powers[1]), 0.0), axis=1, keepdims=True)
        for p in powers
    ]
    place = [jnp.sum(jnp.where(eye, x, 0), axis=1, keepdims=True) for x in place_row]
    col_at = iota((tokens, ep_n * TILE), 1)
    picks = jnp.concatenate(
        [
            jnp.where(col_at - f * cap == place[c], 1.0, 0.0)
            for f in range(back_folds)
            for c in range(2)
        ],
        axis=0,
    ).astype(jnp.bfloat16)

    drain(back_in.at[pl.ds(0, total - 1)], back_recv)
    drain(back_in.at[0], own_sem)
    for h in range(dp_n):
        tiles = back_in[h * ep_n : (h + 1) * ep_n].reshape(ep_n * TILE, back_cols)
        picked = dot(picks, tiles)
        for f in range(back_folds):
            at = 2 * f * tokens
            cols = slice((h * back_folds + f) * back_cols, (h * back_folds + f + 1) * back_cols)
            mixed[:, cols] = (
                gates[0] * picked[at : at + tokens] + gates[1] * picked[at + tokens : at + 2 * tokens]
            ).astype(jnp.bfloat16)

    drain(disp.at[pl.ds(0, ep_n - 1)], disp_send)
    if dp_n > 1:
        drain(rows.at[pl.ds(0, (dp_n - 1) * ep_n)], relay_send)
        drain(hid.at[pl.ds(0, WAVES * (dp_n - 1))], hid_send)
    drain(back_out.at[pl.ds(0, total - 1)], back_send)


def shards(dp_n, ep_n, *args):
    (hidden_in, expert_ids, route_logits, first_weight, second_weight,
     queries, span_keys, span_values, cache_keys, cache_values, valid_frames) = args
    tokens, width = hidden_in.shape
    cap = max(2, 8 * tokens // (3 * ep_n))
    _, _, units = first_weight.shape
    _, all_units, cols = second_weight.shape
    folds = TILE // cap
    back_folds = min(folds, cols // 128)
    slots = dp_n * (ep_n // WAVES) * cap
    bf16 = jnp.bfloat16
    vmem, hbm = pl.BlockSpec(memory_space=pltpu.VMEM), pl.BlockSpec(memory_space=pltpu.HBM)
    dma = pltpu.SemaphoreType.DMA
    total = dp_n * ep_n
    streamed = (
        expert_ids.T, route_logits.T, hidden_in,
        queries, span_keys, span_values, cache_keys[0], cache_values[0],
        first_weight[0], second_weight[0],
    )
    return pl.pallas_call(
        functools.partial(kernel, dp_n, ep_n, cap, back_folds),
        out_shape=(
            jax.ShapeDtypeStruct((tokens, width), bf16),
            jax.ShapeDtypeStruct(queries.shape, bf16),
        ),
        in_specs=[pl.BlockSpec(memory_space=pltpu.SMEM)] + [hbm] * len(streamed),
        out_specs=(vmem, vmem),
        scratch_shapes=[
            pltpu.VMEM((2, tokens), jnp.int32),
            pltpu.VMEM((ep_n, tokens), jnp.float32),
            pltpu.VMEM((tokens, width), bf16),
            pltpu.VMEM((width, units), bf16),
            pltpu.VMEM((all_units, cols), bf16),
            pltpu.VMEM(queries.shape, bf16),
            pltpu.VMEM(span_keys.shape, bf16),
            pltpu.VMEM(span_values.shape, bf16),
            pltpu.VMEM(cache_keys.shape[1:], bf16),
            pltpu.VMEM(cache_values.shape[1:], bf16),
            pltpu.VMEM((ep_n, TILE, width // folds), bf16),
            pltpu.VMEM((total, TILE, width // folds), bf16),
            pltpu.VMEM((folds, slots, width // folds), bf16),
            pltpu.VMEM((WAVES * dp_n, slots, units), bf16),
            pltpu.VMEM((back_folds, slots, cols // back_folds), bf16),
            pltpu.VMEM((total, TILE, cols // back_folds), bf16),
            pltpu.VMEM((total, TILE, cols // back_folds), bf16),
            dma((len(streamed),)),
            dma(()),
            dma((ep_n,)),
            dma(()),
            dma((WAVES * dp_n,)),
            dma(()),
            dma((WAVES * dp_n,)),
            dma(()),
            dma(()),
            dma(()),
        ],
        compiler_params=pltpu.CompilerParams(
            collective_id=0, has_side_effects=True, vmem_limit_bytes=48 * 1024 * 1024
        ),
    )(
        valid_frames,
        *[pltpu.with_memory_space_constraint(x, pltpu.HBM) for x in streamed],
    )


def solution(mesh):
    tokens = P(("dp", "ep"), None)
    weights = P("ep", None, "dp")
    cache = P(("dp", "ep"), None, None)
    return jax.shard_map(
        functools.partial(shards, mesh.shape["dp"], mesh.shape["ep"]),
        mesh=mesh,
        in_specs=(
            tokens, tokens, tokens, weights, weights, tokens, tokens, tokens, cache, cache,
            P(("dp", "ep")),
        ),
        out_specs=(tokens, tokens),
        check_vma=False,
    )
```

time: 41.2 us -> 43.8 us (1.063)
  Pallas kernels: 38.4 us -> 41 us
    pallas_call x1, Pallas kernels: 38.4 us -> 41 us  [shards(): pl.pallas_call(functools.partial(kernel, dp_n, ep_n, cap, back_folds), ou...]
where the time goes in v1:
time: 43.8 us; the launch traced here: 43.6 us
  Pallas kernels  41 us (94%)
  local copies, waits for them, and re-layouts  1.32 us (3%)
  between operations  1.29 us (3%)
    pallas_call x1, Pallas kernels, shards(): pl.pallas_call(functools.partial(kernel, dp_n, ep_n, cap, back_folds), ou...  41 us
    unnamed x2, local copies, waits for them, and re-layouts  1.32 us

profile of v1, /device:TPU:0, one launch (start us, length us, event | category | flops | bytes accessed | tf_op | source)
XLA Modules:
  0.0 43.6 jit_solution(14032406778311698622)
XLA Ops:
  1.3 41.0 %shard_map.122 = (bf16[24,4096]{1,0:T(8,128)(2,1)S(1)}, bf16[24,2048]{1,0:T(8,128)(2,1)S(1)}) custom-call(s32[1]{0:T(128)S(6)} %copy.15.frames, s32[2,24]{1,0:T(2,128)} %bitcast.11, f32[16,24]{1,0:T(8,128)} %bitcast.10, bf16[24,4096]{1,0:T(8,128)(2,1)} %hidden_hbm.1, bf16[24,2048]{1,0:T(8,128)(2,1)} %q_hbm.1, bf16[24,2048]{1,0:T(8,128)(2,1)} %k_hbm.1, ...), custom_call_target="tpu_custom_call" | custom-call | tf_op jit(solution)/shard_map/pallas_call | solution.py:367
  42.3 0.7 %copy.16 = bf16[24,4096]{1,0:T(8,128)(2,1)} copy(bf16[24,4096]{1,0:T(8,128)(2,1)S(1)} %get-tuple-element.4) | data formatting | bytes 393216
  43.0 0.6 %copy.17 = bf16[24,2048]{1,0:T(8,128)(2,1)} copy(bf16[24,2048]{1,0:T(8,128)(2,1)S(1)} %get-tuple-element.5) | data formatting | bytes 196608

commit v2 on v1

v2 whole, which is shorter than its diff:
```python
import functools
import math

import jax
import jax.numpy as jnp
from jax import lax
from jax.experimental import pallas as pl
from jax.experimental.pallas import tpu as pltpu
from jax.sharding import PartitionSpec as P

HEAD_DIM = 128
FRAME_TOK = 24
TILE = 16
WAVES = 4
BLOCK = 16
MESH = pl.DeviceIdType.MESH


def iota(shape, axis):
    return lax.broadcasted_iota(jnp.int32, shape, axis)


def as_bf16(mask):
    return jnp.where(mask, 1.0, 0.0).astype(jnp.bfloat16)


def log2(n):
    return n.bit_length() - 1


def fold_map(shape, long_axis, group, cap):
    long, tiled = iota(shape, long_axis), iota(shape, 1 - long_axis)
    fold = long >> log2(group * cap)
    source = (long & (group * cap - 1)) >> log2(cap)
    slot = long & (cap - 1)
    return as_bf16(tiled == source * TILE + fold * cap + slot)


def dot(a, b):
    return jnp.dot(a, b, preferred_element_type=jnp.float32)


def drain(view, sem):
    pltpu.make_async_copy(view, view, sem).wait()


def loop(low, high, body):
    if high - low <= 8:
        for i in range(low, high):
            body(i)
    else:
        lax.fori_loop(low, high, lambda i, carry: (body(i), carry)[1], 0)


def attend(q, k, v, ck, cv, frames, out, head):
    cache_len = ck.shape[0]
    scale = 1.0 / math.sqrt(HEAD_DIM)
    usable = (iota((1, cache_len), 1) // FRAME_TOK) < frames
    contract = (((1,), (1,)), ((), ()))
    cols = slice(head * HEAD_DIM, (head + 1) * HEAD_DIM)
    query = q[:, cols]
    old = lax.dot_general(query, ck[:, cols], contract, preferred_element_type=jnp.float32)
    new = lax.dot_general(query, k[:, cols], contract, preferred_element_type=jnp.float32)
    old = jnp.where(usable, old * scale, -1e30)
    new = new * scale
    top = jnp.maximum(
        jnp.max(old, axis=1, keepdims=True), jnp.max(new, axis=1, keepdims=True)
    )
    old = jnp.exp(old - top)
    new = jnp.exp(new - top)
    total = jnp.sum(old, axis=1, keepdims=True) + jnp.sum(new, axis=1, keepdims=True)
    old = (old / total).astype(jnp.bfloat16)
    new = (new / total).astype(jnp.bfloat16)
    out[:, cols] = (dot(old, cv[:, cols]) + dot(new, v[:, cols])).astype(jnp.bfloat16)


def kernel(
    dp_n, ep_n, cap, back_folds,
    frames, ids_hbm, logits_hbm, hidden_hbm,
    q_hbm, k_hbm, v_hbm, ck_hbm, cv_hbm, w1_hbm, w2_hbm,
    mixed, attended,
    ids, logits, hidden, w1, w2, q, k, v, ck, cv,
    disp, rows, xs, hid, ys, back_out, mid_in, back_in,
    load_sem, disp_send, disp_recv, relay_send, relay_recv,
    hid_send, hid_recv, mid_send, mid_recv, back_send, back_recv, own_sem,
):
    d, me = lax.axis_index("dp"), lax.axis_index("ep")
    tokens = hidden.shape[0]
    folds = TILE // cap
    fold_cols = disp.shape[2]
    back_cols = back_in.shape[2]
    total = dp_n * ep_n
    quarter, half = ep_n // 4, ep_n // 2
    wave, per = ep_n // WAVES, half // WAVES
    units = hid.shape[1] // dp_n

    bits = [lax.rem(lax.div(me, jnp.int32(1 << b)), jnp.int32(2)) for b in range(log2(ep_n))]
    inner = bits[-2] + bits[-1] - 2 * bits[-2] * bits[-1]
    others = [lax.rem(d + j, jnp.int32(dp_n)) for j in range(1, dp_n)]

    def partner(off):
        both = jnp.int32(0)
        for b, bit in enumerate(bits):
            both = both + (bit * ((off // (1 << b)) % 2)) * (1 << b)
        return me + off - 2 * both

    def far_target(g, i):
        return half + (i // per) * quarter + g * per + i % per

    def target(part, i):
        if part == 0:
            return (1 - inner) * far_target(0, i) + inner * (quarter + i)
        if part == 1:
            return i
        if part == 2:
            return (1 - inner) * (quarter + i) + inner * far_target(0, i)
        return far_target(1, i)

    def landing(off):
        lo = off % quarter
        far = off // half
        w = far * (2 * (lo // per) + inner) + (1 - far) * (off // per)
        return w * wave + far * per + lo % per

    def source(w, far, i):
        if not far:
            return w * per + i
        side = inner if w % 2 else 1 - inner
        return half + side * quarter + (w // 2) * per + i - per

    barrier = pltpu.get_barrier_semaphore()

    loads = [
        pltpu.make_async_copy(src, dst, load_sem.at[i])
        for i, (src, dst) in enumerate(
            [
                (ids_hbm, ids), (logits_hbm, logits), (hidden_hbm, hidden),
                (q_hbm, q), (k_hbm, k), (v_hbm, v), (ck_hbm, ck), (cv_hbm, cv),
                (w1_hbm, w1), (w2_hbm, w2),
            ]
        )
    ]
    for load in loads[:3]:
        load.start()

    def greet(off):
        pl.semaphore_signal(
            barrier, inc=1, device_id={"dp": d, "ep": partner(off)}, device_id_type=MESH
        )

    for plane in others:
        pl.semaphore_signal(barrier, inc=1, device_id={"dp": plane, "ep": me}, device_id_type=MESH)
    loop(1, ep_n, lambda i: greet(ep_n - i))
    for load in loads[3:]:
        load.start()
    for load in loads[:3]:
        load.wait()

    experts = iota((ep_n, tokens), 0)
    named = [experts == ids[c : c + 1, :] for c in range(2)]
    count = as_bf16(named[0] | named[1])
    earlier = as_bf16(iota((tokens, tokens), 0) < iota((tokens, tokens), 1))
    before = dot(count, earlier)
    eye = iota((tokens, tokens), 0) == iota((tokens, tokens), 1)
    place_row, back_row = [], []
    for c in range(2):
        slot = jnp.sum(jnp.where(named[c], before, 0.0), axis=0, keepdims=True).astype(jnp.int32)
        off = ids[c : c + 1, :] ^ me
        lo = off & (quarter - 1)
        side = (off >> log2(quarter)) & 1
        g = lo >> log2(per)
        far = (3 * g + (1 - g) * 2 * inner) * quarter + side * per + (lo & (per - 1))
        beside = lo + jnp.where(side > 0, 2 * (1 - inner), 1) * quarter
        at = jnp.where(off < half, beside, far)
        back_row.append(off * TILE + slot)
        place_row.append(at * TILE + slot)

    row_at = iota((quarter * TILE, tokens), 0)

    def pick(part):
        base = part * quarter
        pickers = [
            as_bf16(
                (row_at + (base * TILE - f * cap) == place_row[0])
                | (row_at + (base * TILE - f * cap) == place_row[1])
            )
            for f in range(folds)
        ]
        step = min(fold_cols, 256)
        for at in range(0, fold_cols, step):
            acc = dot(pickers[0], hidden[:, at : at + step])
            for f in range(1, folds):
                acc += dot(pickers[f], hidden[:, f * fold_cols + at : f * fold_cols + at + step])
            disp[base : base + quarter, :, at : at + step] = acc.astype(jnp.bfloat16).reshape(
                quarter, TILE, step
            )

    def pass_on(g, p, chunk):
        for plane in others:
            pltpu.make_async_remote_copy(
                src_ref=chunk,
                dst_ref=rows.at[d * ep_n + p],
                send_sem=relay_send,
                recv_sem=relay_recv.at[g * dp_n + d],
                device_id={"dp": plane, "ep": me},
                device_id_type=MESH,
            ).start()

    def dispatch(part):
        def send(i):
            off = target(part, i)
            p = landing(off)
            pltpu.make_async_remote_copy(
                src_ref=disp.at[part * quarter + i],
                dst_ref=rows.at[d * ep_n + p],
                send_sem=disp_send,
                recv_sem=disp_recv.at[p],
                device_id={"dp": d, "ep": partner(off)},
                device_id_type=MESH,
            ).start()

        if part == 1:
            pltpu.make_async_copy(disp.at[quarter], rows.at[d * ep_n], disp_recv.at[0]).start()
            pass_on(0, 0, disp.at[quarter])
        loop(1 if part == 1 else 0, quarter, send)

    def relay(w, far):
        def one(p):
            chunk = rows.at[d * ep_n + p]
            drain(chunk, disp_recv.at[p])
            pass_on(w, p, chunk)

        low = far * per
        if w == 0 and not far:
            drain(rows.at[d * ep_n], disp_recv.at[0])
            low = 1
        loop(low, (1 + far) * per, lambda i: one(w * wave + i))

    def blocks(g):
        at, n = g * wave, wave
        size = min(BLOCK, dp_n * n)
        for b in range(0, dp_n * n, size):
            if size < n:
                yield b, size, [(b // n * ep_n + at + b % n, size)]
            else:
                yield b, size, [((b // n + j) * ep_n + at, n) for j in range(size // n)]

    def first(g):
        at, n = g * wave, wave
        height = dp_n * n * cap
        for plane in others:
            drain(rows.at[pl.ds(plane * ep_n + at, n)], relay_recv.at[g * dp_n + plane])
        for b, size, parts in blocks(g):
            unfold = fold_map((folds * size * cap, size * TILE), 0, size, cap)
            tiles = jnp.concatenate(
                [rows[lo : lo + m].reshape(m * TILE, fold_cols) for lo, m in parts], axis=0
            )
            flat = dot(unfold, tiles).astype(jnp.bfloat16)
            for f in range(folds):
                xs[b * cap : (b + size) * cap, f * fold_cols : (f + 1) * fold_cols] = flat[f * size * cap : (f + 1) * size * cap]
        acc = dot(xs[...], w1[...])
        here = (pl.ds(g * height, height), pl.ds(pl.multiple_of(d * units, 128), units))
        hid[here] = jax.nn.gelu(acc, approximate=True).astype(jnp.bfloat16)
        for plane in others:
            pltpu.make_async_remote_copy(
                src_ref=hid.at[here],
                dst_ref=hid.at[here],
                send_sem=hid_send,
                recv_sem=hid_recv.at[g * dp_n + d],
                device_id={"dp": plane, "ep": me},
                device_id_type=MESH,
            ).start()

    def hid_wait(g):
        height = dp_n * wave * cap
        for plane in others:
            part = hid.at[pl.ds(g * height, height), pl.ds(pl.multiple_of(plane * units, 128), units)]
            drain(part, hid_recv.at[g * dp_n + plane])

    def second(g):
        at, n = g * wave, wave
        height = dp_n * n * cap
        ys[...] = dot(hid[g * height : (g + 1) * height, :], w2[...]).astype(jnp.bfloat16)
        for b, size, parts in blocks(g):
            refold = fold_map((size * TILE, back_folds * size * cap), 1, size, cap)
            flat = jnp.concatenate(
                [
                    ys[b * cap : (b + size) * cap, f * back_cols : (f + 1) * back_cols]
                    for f in range(back_folds)
                ],
                axis=0,
            )
            tiles = dot(refold, flat).astype(jnp.bfloat16).reshape(size, TILE, back_cols)
            done = 0
            for lo, m in parts:
                back_out[lo : lo + m] = tiles[done : done + m]
                done += m
        give_back(g, back_out, d, d)
        if g == 0:
            pltpu.make_async_copy(back_out.at[d * ep_n], back_in.at[d * ep_n], own_sem).start()

    def give_back(g, tiles, plane, origin):
        at, n = g * wave, wave

        def give(far, i):
            off = source(g, far, i)
            pltpu.make_async_remote_copy(
                src_ref=tiles.at[plane * ep_n + at + i],
                dst_ref=back_in.at[origin * ep_n + off],
                send_sem=back_send,
                recv_sem=back_recv,
                device_id={"dp": d if tiles is mid_in else plane, "ep": partner(off)},
                device_id_type=MESH,
            ).start()

        loop(per, n, functools.partial(give, True))
        loop(1 if g == 0 else 0, per, functools.partial(give, False))

    def straight(g):
        for plane in others:
            give_back(g, back_out, plane, d)
            if g == 0:
                hand_over(plane)

    def hand_over(plane):
        pltpu.make_async_remote_copy(
            src_ref=back_out.at[plane * ep_n],
            dst_ref=back_in.at[d * ep_n],
            send_sem=back_send,
            recv_sem=back_recv,
            device_id={"dp": plane, "ep": me},
            device_id_type=MESH,
        ).start()

    def span(g, plane):
        at, n = g * wave, wave
        skip = 1 if g == 0 else 0
        return pl.ds(plane * ep_n + at + skip, n - skip)

    def across(g):
        for plane in others:
            pltpu.make_async_remote_copy(
                src_ref=back_out.at[span(g, plane)],
                dst_ref=mid_in.at[span(g, d)],
                send_sem=mid_send,
                recv_sem=mid_recv.at[g * dp_n + d],
                device_id={"dp": plane, "ep": me},
                device_id_type=MESH,
            ).start()
            if g == 0:
                hand_over(plane)
        bridged.append(g)

    def bring(g):
        for plane in others:
            drain(mid_in.at[span(g, plane)], mid_recv.at[g * dp_n + plane])
            give_back(g, mid_in, plane, plane)

    bridged = []
    waiting = list(range(q.shape[1] // HEAD_DIM))

    def heads(n):
        for _ in range(min(n, len(waiting))):
            attend(q, k, v, ck, cv, frames[0], attended, waiting.pop(0))

    pick(0)
    pl.semaphore_wait(barrier, ep_n + dp_n - 2)
    dispatch(0)
    for part in range(1, 4):
        pick(part)
        dispatch(part)
    for load in loads[3:8]:
        load.wait()
    heads(1)
    relay(0, 0)
    heads(1)
    relay(1, 0)
    heads(2)
    relay(0, 1)
    relay(2, 0)
    heads(2)
    loads[8].wait()
    relay(1, 1)
    first(0)
    relay(3, 0)
    relay(2, 1)
    first(1)
    loads[9].wait()
    hid_wait(0)
    second(0)
    relay(3, 1)
    straight(0)
    first(2)
    hid_wait(1)
    second(1)
    first(3)
    straight(1)
    hid_wait(2)
    second(2)
    hid_wait(3)
    straight(2)
    second(3)
    straight(3)
    heads(16)

    chosen = [
        jnp.sum(jnp.where(named[c], logits[...], 0.0), axis=0, keepdims=True) for c in range(2)
    ]
    top = jnp.maximum(chosen[0], chosen[1])
    powers = [jnp.exp(x - top) for x in chosen]
    gates = [
        jnp.sum(jnp.where(eye, p / (powers[0] + powers[1]), 0.0), axis=1, keepdims=True)
        for p in powers
    ]
    place = [jnp.sum(jnp.where(eye, x, 0), axis=1, keepdims=True) for x in back_row]
    col_at = iota((tokens, ep_n * TILE), 1)
    picks = jnp.concatenate(
        [
            jnp.where(col_at - f * cap == place[c], 1.0, 0.0)
            for f in range(back_folds)
            for c in range(2)
        ],
        axis=0,
    ).astype(jnp.bfloat16)

    drain(back_in.at[pl.ds(0, total - 1)], back_recv)
    drain(back_in.at[0], own_sem)
    for h in range(dp_n):
        tiles = back_in[h * ep_n : (h + 1) * ep_n].reshape(ep_n * TILE, back_cols)
        picked = dot(picks, tiles)
        for f in range(back_folds):
            at = 2 * f * tokens
            cols = slice((h * back_folds + f) * back_cols, (h * back_folds + f + 1) * back_cols)
            mixed[:, cols] = (
                gates[0] * picked[at : at + tokens] + gates[1] * picked[at + tokens : at + 2 * tokens]
            ).astype(jnp.bfloat16)

    drain(disp.at[pl.ds(0, ep_n - 1)], disp_send)
    if dp_n > 1:
        drain(rows.at[pl.ds(0, (dp_n - 1) * ep_n)], relay_send)
        drain(hid.at[:, pl.ds(0, (dp_n - 1) * units)], hid_send)
        passed = sum(wave - (g == 0) for g in bridged)
        drain(mid_in.at[pl.ds(0, (dp_n - 1) * passed)], mid_send)
    drain(back_out.at[pl.ds(0, total - 1)], back_send)


def shards(dp_n, ep_n, *args):
    (hidden_in, expert_ids, route_logits, first_weight, second_weight,
     queries, span_keys, span_values, cache_keys, cache_values, valid_frames) = args
    tokens, width = hidden_in.shape
    cap = max(2, 8 * tokens // (3 * ep_n))
    _, _, units = first_weight.shape
    _, all_units, cols = second_weight.shape
    folds = TILE // cap
    back_folds = min(folds, cols // 128)
    bf16 = jnp.bfloat16
    vmem, hbm = pl.BlockSpec(memory_space=pltpu.VMEM), pl.BlockSpec(memory_space=pltpu.HBM)
    dma = pltpu.SemaphoreType.DMA
    total = dp_n * ep_n
    height = total * cap
    streamed = (
        expert_ids.T, route_logits.T, hidden_in,
        queries, span_keys, span_values, cache_keys[0], cache_values[0],
        first_weight[0], second_weight[0],
    )
    return pl.pallas_call(
        functools.partial(kernel, dp_n, ep_n, cap, back_folds),
        out_shape=(
            jax.ShapeDtypeStruct((tokens, width), bf16),
            jax.ShapeDtypeStruct(queries.shape, bf16),
        ),
        in_specs=[pl.BlockSpec(memory_space=pltpu.SMEM)] + [hbm] * len(streamed),
        out_specs=(vmem, vmem),
        scratch_shapes=[
            pltpu.VMEM((2, tokens), jnp.int32),
            pltpu.VMEM((ep_n, tokens), jnp.float32),
            pltpu.VMEM((tokens, width), bf16),
            pltpu.VMEM((width, units), bf16),
            pltpu.VMEM((all_units, cols), bf16),
            pltpu.VMEM(queries.shape, bf16),
            pltpu.VMEM(span_keys.shape, bf16),
            pltpu.VMEM(span_values.shape, bf16),
            pltpu.VMEM(cache_keys.shape[1:], bf16),
            pltpu.VMEM(cache_values.shape[1:], bf16),
            pltpu.VMEM((ep_n, TILE, width // folds), bf16),
            pltpu.VMEM((total, TILE, width // folds), bf16),
            pltpu.VMEM((height // WAVES, width), bf16),
            pltpu.VMEM((height, dp_n * units), bf16),
            pltpu.VMEM((height // WAVES, cols), bf16),
            pltpu.VMEM((total, TILE, cols // back_folds), bf16),
            pltpu.VMEM((total, TILE, cols // back_folds), bf16),
            pltpu.VMEM((total, TILE, cols // back_folds), bf16),
            dma((len(streamed),)),
            dma(()),
            dma((ep_n,)),
            dma(()),
            dma((WAVES * dp_n,)),
            dma(()),
            dma((WAVES * dp_n,)),
            dma(()),
            dma((WAVES * dp_n,)),
            dma(()),
            dma(()),
            dma(()),
        ],
        compiler_params=pltpu.CompilerParams(
            collective_id=0, has_side_effects=True, vmem_limit_bytes=44 * 1024 * 1024
        ),
    )(
        valid_frames,
        *[pltpu.with_memory_space_constraint(x, pltpu.HBM) for x in streamed],
    )


def solution(mesh):
    tokens = P(("dp", "ep"), None)
    weights = P("ep", None, "dp")
    cache = P(("dp", "ep"), None, None)
    return jax.shard_map(
        functools.partial(shards, mesh.shape["dp"], mesh.shape["ep"]),
        mesh=mesh,
        in_specs=(
            tokens, tokens, tokens, weights, weights, tokens, tokens, tokens, cache, cache,
            P(("dp", "ep")),
        ),
        out_specs=(tokens, tokens),
        check_vma=False,
    )
```

time: 43.8 us -> 38 us (0.87)
  Pallas kernels: 41 us -> 35.2 us
    pallas_call x1, Pallas kernels: 41 us -> 35.2 us  [shards(): pl.pallas_call(functools.partial(kernel, dp_n, ep_n, cap, back_folds), ou...]
where the time goes in v2:
time: 38 us; the launch traced here: 37.8 us
  Pallas kernels  35.2 us (93%)
  local copies, waits for them, and re-layouts  1.32 us (3%)
  between operations  1.29 us (3%)
    pallas_call x1, Pallas kernels, shards(): pl.pallas_call(functools.partial(kernel, dp_n, ep_n, cap, back_folds), ou...  35.2 us
    unnamed x2, local copies, waits for them, and re-layouts  1.32 us

profile of v2, /device:TPU:0, one launch (start us, length us, event | category | flops | bytes accessed | tf_op | source)
XLA Modules:
  0.0 37.8 jit_solution(9430899035538563933)
XLA Ops:
  1.3 35.2 %shard_map.122 = (bf16[24,4096]{1,0:T(8,128)(2,1)S(1)}, bf16[24,2048]{1,0:T(8,128)(2,1)S(1)}) custom-call(s32[1]{0:T(128)S(6)} %copy.15.frames, s32[2,24]{1,0:T(2,128)} %bitcast.11, f32[16,24]{1,0:T(8,128)} %bitcast.10, bf16[24,4096]{1,0:T(8,128)(2,1)} %hidden_hbm.1, bf16[24,2048]{1,0:T(8,128)(2,1)} %q_hbm.1, bf16[24,2048]{1,0:T(8,128)(2,1)} %k_hbm.1, ...), custom_call_target="tpu_custom_call" | custom-call | tf_op jit(solution)/shard_map/pallas_call | solution.py:466
  36.5 0.7 %copy.16 = bf16[24,4096]{1,0:T(8,128)(2,1)} copy(bf16[24,4096]{1,0:T(8,128)(2,1)S(1)} %get-tuple-element.4) | data formatting | bytes 393216
  37.2 0.6 %copy.17 = bf16[24,2048]{1,0:T(8,128)(2,1)} copy(bf16[24,2048]{1,0:T(8,128)(2,1)S(1)} %get-tuple-element.5) | data formatting | bytes 196608

commit v3 on v2

--- a/solution.py
+++ b/solution.py
@@ -11,7 +11,9 @@
 HEAD_DIM = 128
 FRAME_TOK = 24
 TILE = 16
-WAVES = 4
+MICRO = 8
+GROUPS = ((0, 1), (1, 1), (2, 2), (4, 2), (6, 2))
+NEAR = (0, 1, 4, 5, 6, 7, 2, 3)
 BLOCK = 16
 MESH = pl.DeviceIdType.MESH
 
@@ -91,7 +93,10 @@
     back_cols = back_in.shape[2]
     total = dp_n * ep_n
     quarter, half = ep_n // 4, ep_n // 2
-    wave, per = ep_n // WAVES, half // WAVES
+    wave, per = ep_n // MICRO, half // MICRO
+    starts = [m * wave for m, _ in GROUPS]
+    counts = [n * wave for _, n in GROUPS]
+    group_of = [g for g, (_, n) in enumerate(GROUPS) for _ in range(n)]
     units = hid.shape[1] // dp_n
 
     bits = [lax.rem(lax.div(me, jnp.int32(1 << b)), jnp.int32(2)) for b in range(log2(ep_n))]
@@ -105,7 +110,8 @@
         return me + off - 2 * both
 
     def far_target(g, i):
-        return half + (i // per) * quarter + g * per + i % per
+        side = i // per % 2
+        return half + side * quarter + g * 2 * per + i // (2 * per) * per + i % per
 
     def target(part, i):
         if part == 0:
@@ -119,14 +125,17 @@
     def landing(off):
         lo = off % quarter
         far = off // half
-        w = far * (2 * (lo // per) + inner) + (1 - far) * (off // per)
-        return w * wave + far * per + lo % per
-
-    def source(w, far, i):
+        block = off // per
+        turn = block // 2 % 2 * (1 - block // 4)
+        near = (block - block // 4 * 2 + turn * 4) * wave + off % per
+        micro = lo // (2 * per) * 4 + inner * 2 + lo // per % 2
+        return far * (micro * wave + per + lo % per) + (1 - far) * near
+
+    def source(micro, far, i):
         if not far:
-            return w * per + i
-        side = inner if w % 2 else 1 - inner
-        return half + side * quarter + (w // 2) * per + i - per
+            return NEAR[micro] * per + i
+        side = inner if micro // 2 % 2 else 1 - inner
+        return half + side * quarter + micro // 4 * 2 * per + micro % 2 * per + i
 
     barrier = pltpu.get_barrier_semaphore()
 
@@ -168,8 +177,9 @@
         off = ids[c : c + 1, :] ^ me
         lo = off & (quarter - 1)
         side = (off >> log2(quarter)) & 1
-        g = lo >> log2(per)
-        far = (3 * g + (1 - g) * 2 * inner) * quarter + side * per + (lo & (per - 1))
+        g = lo >> log2(2 * per)
+        far = (3 * g + (1 - g) * 2 * inner) * quarter
+        far += ((lo >> log2(per)) & 1) * 2 * per + side * per + (lo & (per - 1))
         beside = lo + jnp.where(side > 0, 2 * (1 - inner), 1) * quarter
         at = jnp.where(off < half, beside, far)
         back_row.append(off * TILE + slot)
@@ -224,20 +234,22 @@
             pass_on(0, 0, disp.at[quarter])
         loop(1 if part == 1 else 0, quarter, send)
 
-    def relay(w, far):
-        def one(p):
-            chunk = rows.at[d * ep_n + p]
-            drain(chunk, disp_recv.at[p])
-            pass_on(w, p, chunk)
-
-        low = far * per
-        if w == 0 and not far:
-            drain(rows.at[d * ep_n], disp_recv.at[0])
-            low = 1
-        loop(low, (1 + far) * per, lambda i: one(w * wave + i))
+    def relay(low, high, far):
+        for micro in range(low, high):
+            def one(i, micro=micro):
+                p = micro * wave + i
+                chunk = rows.at[d * ep_n + p]
+                drain(chunk, disp_recv.at[p])
+                pass_on(group_of[micro], p, chunk)
+
+            first_one = far * per
+            if micro == 0 and not far:
+                drain(rows.at[d * ep_n], disp_recv.at[0])
+                first_one = 1
+            loop(first_one, (1 + far) * per, one)
 
     def blocks(g):
-        at, n = g * wave, wave
+        at, n = starts[g], counts[g]
         size = min(BLOCK, dp_n * n)
         for b in range(0, dp_n * n, size):
             if size < n:
@@ -246,7 +258,7 @@
                 yield b, size, [((b // n + j) * ep_n + at, n) for j in range(size // n)]
 
     def first(g):
-        at, n = g * wave, wave
+        at, n = starts[g], counts[g]
         height = dp_n * n * cap
         for plane in others:
             drain(rows.at[pl.ds(plane * ep_n + at, n)], relay_recv.at[g * dp_n + plane])
@@ -258,8 +270,8 @@
             flat = dot(unfold, tiles).astype(jnp.bfloat16)
             for f in range(folds):
                 xs[b * cap : (b + size) * cap, f * fold_cols : (f + 1) * fold_cols] = flat[f * size * cap : (f + 1) * size * cap]
-        acc = dot(xs[...], w1[...])
-        here = (pl.ds(g * height, height), pl.ds(pl.multiple_of(d * units, 128), units))
+        acc = dot(xs[:height, :], w1[...])
+        here = (pl.ds(dp_n * at * cap, height), pl.ds(pl.multiple_of(d * units, 128), units))
         hid[here] = jax.nn.gelu(acc, approximate=True).astype(jnp.bfloat16)
         for plane in others:
             pltpu.make_async_remote_copy(
@@ -272,15 +284,16 @@
             ).start()
 
     def hid_wait(g):
-        height = dp_n * wave * cap
-        for plane in others:
-            part = hid.at[pl.ds(g * height, height), pl.ds(pl.multiple_of(plane * units, 128), units)]
+        height, low = dp_n * counts[g] * cap, dp_n * starts[g] * cap
+        for plane in others:
+            part = hid.at[pl.ds(low, height), pl.ds(pl.multiple_of(plane * units, 128), units)]
             drain(part, hid_recv.at[g * dp_n + plane])
 
     def second(g):
-        at, n = g * wave, wave
+        at, n = starts[g], counts[g]
         height = dp_n * n * cap
-        ys[...] = dot(hid[g * height : (g + 1) * height, :], w2[...]).astype(jnp.bfloat16)
+        low = dp_n * at * cap
+        ys[:height, :] = dot(hid[low : low + height, :], w2[...]).astype(jnp.bfloat16)
         for b, size, parts in blocks(g):
             refold = fold_map((size * TILE, back_folds * size * cap), 1, size, cap)
             flat = jnp.concatenate(
@@ -300,12 +313,9 @@
             pltpu.make_async_copy(back_out.at[d * ep_n], back_in.at[d * ep_n], own_sem).start()
 
     def give_back(g, tiles, plane, origin):
-        at, n = g * wave, wave
-
-        def give(far, i):
-            off = source(g, far, i)
+        def give(p, off):
             pltpu.make_async_remote_copy(
-                src_ref=tiles.at[plane * ep_n + at + i],
+                src_ref=tiles.at[plane * ep_n + p],
                 dst_ref=back_in.at[origin * ep_n + off],
                 send_sem=back_send,
                 recv_sem=back_recv,
@@ -313,8 +323,11 @@
                 device_id_type=MESH,
             ).start()
 
-        loop(per, n, functools.partial(give, True))
-        loop(1 if g == 0 else 0, per, functools.partial(give, False))
+        for far in (True, False):
+            for micro in range(GROUPS[g][0], sum(GROUPS[g])):
+                low = 1 if micro == 0 and not far else 0
+                at = micro * wave + far * per
+                loop(low, per, lambda i, m=micro, f=far, a=at: give(a + i, source(m, f, i)))
 
     def straight(g):
         for plane in others:
@@ -333,7 +346,7 @@
         ).start()
 
     def span(g, plane):
-        at, n = g * wave, wave
+        at, n = starts[g], counts[g]
         skip = 1 if g == 0 else 0
         return pl.ds(plane * ep_n + at + skip, n - skip)
 
@@ -372,35 +385,41 @@
     for load in loads[3:8]:
         load.wait()
     heads(1)
-    relay(0, 0)
+    relay(0, 2, 0)
     heads(1)
-    relay(1, 0)
-    heads(2)
-    relay(0, 1)
-    relay(2, 0)
-    heads(2)
+    relay(6, 8, 0)
+    heads(1)
+    relay(0, 1, 1)
+    heads(1)
+    relay(1, 2, 1)
+    heads(1)
+    relay(2, 4, 0)
+    relay(2, 4, 1)
     loads[8].wait()
-    relay(1, 1)
     first(0)
-    relay(3, 0)
-    relay(2, 1)
     first(1)
+    relay(4, 6, 0)
+    relay(4, 6, 1)
+    first(2)
     loads[9].wait()
     hid_wait(0)
     second(0)
-    relay(3, 1)
-    straight(0)
-    first(2)
     hid_wait(1)
     second(1)
+    relay(6, 8, 1)
     first(3)
-    straight(1)
+    straight(0)
     hid_wait(2)
     second(2)
+    first(4)
+    straight(1)
     hid_wait(3)
-    straight(2)
     second(3)
     straight(3)
+    hid_wait(4)
+    second(4)
+    straight(2)
+    straight(4)
     heads(16)
 
     chosen = [
@@ -439,9 +458,22 @@
     if dp_n > 1:
         drain(rows.at[pl.ds(0, (dp_n - 1) * ep_n)], relay_send)
         drain(hid.at[:, pl.ds(0, (dp_n - 1) * units)], hid_send)
-        passed = sum(wave - (g == 0) for g in bridged)
+        passed = sum(counts[g] - (g == 0) for g in bridged)
         drain(mid_in.at[pl.ds(0, (dp_n - 1) * passed)], mid_send)
     drain(back_out.at[pl.ds(0, total - 1)], back_send)
+
+
+def write_out(*refs):
+    *refs, sem = refs
+    half = len(refs) // 2
+    copies = [
+        pltpu.make_async_copy(src, dst, sem.at[i])
+        for i, (src, dst) in enumerate(zip(refs[:half], refs[half:]))
+    ]
+    for copy in copies:
+        copy.start()
+    for copy in copies:
+        copy.wait()
 
 
 def shards(dp_n, ep_n, *args):
@@ -458,12 +490,13 @@
     dma = pltpu.SemaphoreType.DMA
     total = dp_n * ep_n
     height = total * cap
+    tall = max(n for _, n in GROUPS)
     streamed = (
         expert_ids.T, route_logits.T, hidden_in,
         queries, span_keys, span_values, cache_keys[0], cache_values[0],
         first_weight[0], second_weight[0],
     )
-    return pl.pallas_call(
+    results = pl.pallas_call(
         functools.partial(kernel, dp_n, ep_n, cap, back_folds),
         out_shape=(
             jax.ShapeDtypeStruct((tokens, width), bf16),
@@ -484,9 +517,9 @@
             pltpu.VMEM(cache_values.shape[1:], bf16),
             pltpu.VMEM((ep_n, TILE, width // folds), bf16),
             pltpu.VMEM((total, TILE, width // folds), bf16),
-            pltpu.VMEM((height // WAVES, width), bf16),
+            pltpu.VMEM((height * tall // MICRO, width), bf16),
             pltpu.VMEM((height, dp_n * units), bf16),
-            pltpu.VMEM((height // WAVES, cols), bf16),
+            pltpu.VMEM((height * tall // MICRO, cols), bf16),
             pltpu.VMEM((total, TILE, cols // back_folds), bf16),
             pltpu.VMEM((total, TILE, cols // back_folds), bf16),
             pltpu.VMEM((total, TILE, cols // back_folds), bf16),
@@ -494,11 +527,11 @@
             dma(()),
             dma((ep_n,)),
             dma(()),
-            dma((WAVES * dp_n,)),
-            dma(()),
-            dma((WAVES * dp_n,)),
-            dma(()),
-            dma((WAVES * dp_n,)),
+            dma((len(GROUPS) * dp_n,)),
+            dma(()),
+            dma((len(GROUPS) * dp_n,)),
+            dma(()),
+            dma((len(GROUPS) * dp_n,)),
             dma(()),
             dma(()),
             dma(()),
@@ -510,6 +543,13 @@
         valid_frames,
         *[pltpu.with_memory_space_constraint(x, pltpu.HBM) for x in streamed],
     )
+    return pl.pallas_call(
+        write_out,
+        out_shape=tuple(jax.ShapeDtypeStruct(x.shape, x.dtype) for x in results),
+        in_specs=[pl.BlockSpec(memory_space=pl.ANY)] * len(results),
+        out_specs=tuple([hbm] * len(results)),
+        scratch_shapes=[dma((len(results),))],
+    )(*[pltpu.with_memory_space_constraint(x, pltpu.VMEM) for x in results])
 
 
 def solution(mesh):

time: 38 us -> 37 us (0.974)
  local copies, waits for them, and re-layouts: 1.32 us -> 0 us
    unnamed x2 -> x0, local copies, waits for them, and re-layouts: 1.32 us -> none
    pallas_call x0 -> x1, Pallas kernels: none -> 0.72 us  [shards(): pl.pallas_call(write_out, out_shape=tuple((jax.ShapeDtypeStruct(x.shape,...]
    pallas_call x1, Pallas kernels: 35.2 us -> 34.8 us  [shards(): pl.pallas_call(functools.partial(kernel, dp_n, ep_n, cap, back_folds), ou...]
where the time goes in v3:
time: 37 us; the launch traced here: 36.8 us
  Pallas kernels  35.5 us (96%)
  between operations  1.29 us (3%)
    pallas_call x1, Pallas kernels, shards(): pl.pallas_call(functools.partial(kernel, dp_n, ep_n, cap, back_folds), ou...  34.8 us

profile of v3, /device:TPU:0, one launch (start us, length us, event | category | flops | bytes accessed | tf_op | source)
XLA Modules:
  0.0 36.8 jit_solution(15305872005105951305)
XLA Ops:
  1.3 34.8 %shard_map.122 = (bf16[24,4096]{1,0:T(8,128)(2,1)S(1)}, bf16[24,2048]{1,0:T(8,128)(2,1)S(1)}) custom-call(s32[1]{0:T(128)S(6)} %copy.13.frames, s32[2,24]{1,0:T(2,128)} %bitcast.11, f32[16,24]{1,0:T(8,128)} %bitcast.10, bf16[24,4096]{1,0:T(8,128)(2,1)} %hidden_hbm.1, bf16[24,2048]{1,0:T(8,128)(2,1)} %q_hbm.1, bf16[24,2048]{1,0:T(8,128)(2,1)} %k_hbm.1, ...), custom_call_target="tpu_custom_call" | custom-call | tf_op jit(solution)/shard_map/pallas_call | solution.py:499
  36.1 0.7 %shard_map.123 = (bf16[24,4096]{1,0:T(8,128)(2,1)}, bf16[24,2048]{1,0:T(8,128)(2,1)}) custom-call(bf16[24,4096]{1,0:T(8,128)(2,1)S(1)} %get-tuple-element.4.refs_0_, bf16[24,2048]{1,0:T(8,128)(2,1)S(1)} %get-tuple-element.5.refs_1_), custom_call_target="tpu_custom_call" | custom-call | tf_op jit(solution)/shard_map/pallas_call | solution.py:546

commit v4 on v3

--- a/solution.py
+++ b/solution.py
@@ -12,7 +12,7 @@
 FRAME_TOK = 24
 TILE = 16
 MICRO = 8
-GROUPS = ((0, 1), (1, 1), (2, 2), (4, 2), (6, 2))
+GROUPS = ((0, 2), (2, 2), (4, 2), (6, 1), (7, 1))
 NEAR = (0, 1, 4, 5, 6, 7, 2, 3)
 BLOCK = 16
 MESH = pl.DeviceIdType.MESH
@@ -82,9 +82,9 @@
     q_hbm, k_hbm, v_hbm, ck_hbm, cv_hbm, w1_hbm, w2_hbm,
     mixed, attended,
     ids, logits, hidden, w1, w2, q, k, v, ck, cv,
-    disp, rows, xs, hid, ys, back_out, mid_in, back_in,
+    disp, rows, xs, hid, ys, back_out, back_in,
     load_sem, disp_send, disp_recv, relay_send, relay_recv,
-    hid_send, hid_recv, mid_send, mid_recv, back_send, back_recv, own_sem,
+    hid_send, hid_recv, back_send, back_recv, own_sem,
 ):
     d, me = lax.axis_index("dp"), lax.axis_index("ep")
     tokens = hidden.shape[0]
@@ -206,12 +206,12 @@
             )
 
     def pass_on(g, p, chunk):
-        for plane in others:
+        for j, plane in enumerate(others):
             pltpu.make_async_remote_copy(
                 src_ref=chunk,
                 dst_ref=rows.at[d * ep_n + p],
                 send_sem=relay_send,
-                recv_sem=relay_recv.at[g * dp_n + d],
+                recv_sem=relay_recv.at[(g + 1) * (dp_n - 1) - 1 - j],
                 device_id={"dp": plane, "ep": me},
                 device_id_type=MESH,
             ).start()
@@ -260,8 +260,8 @@
     def first(g):
         at, n = starts[g], counts[g]
         height = dp_n * n * cap
-        for plane in others:
-            drain(rows.at[pl.ds(plane * ep_n + at, n)], relay_recv.at[g * dp_n + plane])
+        for j, plane in enumerate(others):
+            drain(rows.at[pl.ds(plane * ep_n + at, n)], relay_recv.at[g * (dp_n - 1) + j])
         for b, size, parts in blocks(g):
             unfold = fold_map((folds * size * cap, size * TILE), 0, size, cap)
             tiles = jnp.concatenate(
@@ -273,21 +273,21 @@
         acc = dot(xs[:height, :], w1[...])
         here = (pl.ds(dp_n * at * cap, height), pl.ds(pl.multiple_of(d * units, 128), units))
         hid[here] = jax.nn.gelu(acc, approximate=True).astype(jnp.bfloat16)
-        for plane in others:
+        for j, plane in enumerate(others):
             pltpu.make_async_remote_copy(
                 src_ref=hid.at[here],
                 dst_ref=hid.at[here],
                 send_sem=hid_send,
-                recv_sem=hid_recv.at[g * dp_n + d],
+                recv_sem=hid_recv.at[(g + 1) * (dp_n - 1) - 1 - j],
                 device_id={"dp": plane, "ep": me},
                 device_id_type=MESH,
             ).start()
 
     def hid_wait(g):
         height, low = dp_n * counts[g] * cap, dp_n * starts[g] * cap
-        for plane in others:
+        for j, plane in enumerate(others):
             part = hid.at[pl.ds(low, height), pl.ds(pl.multiple_of(plane * units, 128), units)]
-            drain(part, hid_recv.at[g * dp_n + plane])
+            drain(part, hid_recv.at[g * (dp_n - 1) + j])
 
     def second(g):
         at, n = starts[g], counts[g]
@@ -308,18 +308,18 @@
             for lo, m in parts:
                 back_out[lo : lo + m] = tiles[done : done + m]
                 done += m
-        give_back(g, back_out, d, d)
+        give_back(g, d)
         if g == 0:
             pltpu.make_async_copy(back_out.at[d * ep_n], back_in.at[d * ep_n], own_sem).start()
 
-    def give_back(g, tiles, plane, origin):
+    def give_back(g, plane):
         def give(p, off):
             pltpu.make_async_remote_copy(
-                src_ref=tiles.at[plane * ep_n + p],
-                dst_ref=back_in.at[origin * ep_n + off],
+                src_ref=back_out.at[plane * ep_n + p],
+                dst_ref=back_in.at[d * ep_n + off],
                 send_sem=back_send,
                 recv_sem=back_recv,
-                device_id={"dp": d if tiles is mid_in else plane, "ep": partner(off)},
+                device_id={"dp": plane, "ep": partner(off)},
                 device_id_type=MESH,
             ).start()
 
@@ -331,7 +331,7 @@
 
     def straight(g):
         for plane in others:
-            give_back(g, back_out, plane, d)
+            give_back(g, plane)
             if g == 0:
                 hand_over(plane)
 
@@ -345,31 +345,7 @@
             device_id_type=MESH,
         ).start()
 
-    def span(g, plane):
-        at, n = starts[g], counts[g]
-        skip = 1 if g == 0 else 0
-        return pl.ds(plane * ep_n + at + skip, n - skip)
-
-    def across(g):
-        for plane in others:
-            pltpu.make_async_remote_copy(
-                src_ref=back_out.at[span(g, plane)],
-                dst_ref=mid_in.at[span(g, d)],
-                send_sem=mid_send,
-                recv_sem=mid_recv.at[g * dp_n + d],
-                device_id={"dp": plane, "ep": me},
-                device_id_type=MESH,
-            ).start()
-            if g == 0:
-                hand_over(plane)
-        bridged.append(g)
-
-    def bring(g):
-        for plane in others:
-            drain(mid_in.at[span(g, plane)], mid_recv.at[g * dp_n + plane])
-            give_back(g, mid_in, plane, plane)
-
-    bridged = []
+
     waiting = list(range(q.shape[1] // HEAD_DIM))
 
     def heads(n):
@@ -397,28 +373,28 @@
     relay(2, 4, 1)
     loads[8].wait()
     first(0)
-    first(1)
     relay(4, 6, 0)
     relay(4, 6, 1)
-    first(2)
+    first(1)
     loads[9].wait()
     hid_wait(0)
     second(0)
+    relay(6, 8, 1)
+    first(2)
     hid_wait(1)
+    straight(0)
     second(1)
-    relay(6, 8, 1)
     first(3)
-    straight(0)
+    first(4)
     hid_wait(2)
     second(2)
-    first(4)
+    straight(2)
+    hid_wait(3)
     straight(1)
-    hid_wait(3)
     second(3)
+    hid_wait(4)
     straight(3)
-    hid_wait(4)
     second(4)
-    straight(2)
     straight(4)
     heads(16)
 
@@ -458,8 +434,6 @@
     if dp_n > 1:
         drain(rows.at[pl.ds(0, (dp_n - 1) * ep_n)], relay_send)
         drain(hid.at[:, pl.ds(0, (dp_n - 1) * units)], hid_send)
-        passed = sum(counts[g] - (g == 0) for g in bridged)
-        drain(mid_in.at[pl.ds(0, (dp_n - 1) * passed)], mid_send)
     drain(back_out.at[pl.ds(0, total - 1)], back_send)
 
 
@@ -522,16 +496,13 @@
             pltpu.VMEM((height * tall // MICRO, cols), bf16),
             pltpu.VMEM((total, TILE, cols // back_folds), bf16),
             pltpu.VMEM((total, TILE, cols // back_folds), bf16),
-            pltpu.VMEM((total, TILE, cols // back_folds), bf16),
             dma((len(streamed),)),
             dma(()),
             dma((ep_n,)),
             dma(()),
-            dma((len(GROUPS) * dp_n,)),
+            dma((len(GROUPS) * max(1, dp_n - 1),)),
             dma(()),
-            dma((len(GROUPS) * dp_n,)),
-            dma(()),
-            dma((len(GROUPS) * dp_n,)),
+            dma((len(GROUPS) * max(1, dp_n - 1),)),
             dma(()),
             dma(()),
             dma(()),

time: 37 us -> 36.5 us (0.986)
  Pallas kernels: 35.5 us -> 35 us
    pallas_call x1, Pallas kernels: 34.8 us -> 34.3 us  [shards(): pl.pallas_call(functools.partial(kernel, dp_n, ep_n, cap, back_folds), ou...]
where the time goes in v4:
time: 36.5 us; the launch traced here: 36.3 us
  Pallas kernels  35 us (96%)
  between operations  1.29 us (4%)
    pallas_call x1, Pallas kernels, shards(): pl.pallas_call(functools.partial(kernel, dp_n, ep_n, cap, back_folds), ou...  34.3 us

profile of v4, /device:TPU:0, one launch (start us, length us, event | category | flops | bytes accessed | tf_op | source)
XLA Modules:
  0.0 36.3 jit_solution(9463908072716926653)
XLA Ops:
  1.3 34.3 %shard_map.122 = (bf16[24,4096]{1,0:T(8,128)(2,1)S(1)}, bf16[24,2048]{1,0:T(8,128)(2,1)S(1)}) custom-call(s32[1]{0:T(128)S(6)} %copy.13.frames, s32[2,24]{1,0:T(2,128)} %bitcast.11, f32[16,24]{1,0:T(8,128)} %bitcast.10, bf16[24,4096]{1,0:T(8,128)(2,1)} %hidden_hbm.1, bf16[24,2048]{1,0:T(8,128)(2,1)} %q_hbm.1, bf16[24,2048]{1,0:T(8,128)(2,1)} %k_hbm.1, ...), custom_call_target="tpu_custom_call" | custom-call | tf_op jit(solution)/shard_map/pallas_call | solution.py:473
  35.6 0.7 %shard_map.123 = (bf16[24,4096]{1,0:T(8,128)(2,1)}, bf16[24,2048]{1,0:T(8,128)(2,1)}) custom-call(bf16[24,4096]{1,0:T(8,128)(2,1)S(1)} %get-tuple-element.4.refs_0_, bf16[24,2048]{1,0:T(8,128)(2,1)S(1)} %get-tuple-element.5.refs_1_), custom_call_target="tpu_custom_call" | custom-call | tf_op jit(solution)/shard_map/pallas_call | solution.py:517
